TPU v7x, 32 devices: a whole 2x2x4 slice. The times are simulated.
32 devices in a mesh: level: 4 (over z), dev: 8 (over y, x, core).
Axes of the slice: x: 2, y: 2, z: 4, core: 2. Of those that a mesh axis runs over, the one named last changes fastest.
Arguments:
- fields: float32 [4, 128, 12, 128], P('level', 'dev'), may hold values from -6 to 6
- own_src: int32 [4, 128], P('level', 'dev'), may hold values from 0 to 15
- own_weight: bfloat16 [4, 128, 128, 128], P('level', 'dev'), may hold values from 0 to 1, as said below
- send_block: int32 [4, 8, 8, 2], P('level', 'dev'), may hold values from 0 to 15
- send_target: int32 [4, 8, 8, 2], P('level', 'dev'), may hold values from 0 to 15
- send_count: int32 [4, 8, 8], P('level', 'dev'), may hold values from 0 to 2, as said below
- send_weight: bfloat16 [4, 8, 8, 2, 128, 128], P('level', 'dev'), may hold values from 0 to 1, as said below
- left_block: int32 [4, 8, 4, 2], P('level', 'dev'), may hold values from 0 to 15
- left_target: int32 [4, 8, 4, 2], P('level', 'dev'), may hold values from 0 to 15
- left_count: int32 [4, 8, 4], P('level', 'dev'), may hold values from 0 to 2, as said below
- left_weight: bfloat16 [4, 8, 4, 2, 128, 128], P('level', 'dev'), may hold values from 0 to 1, as said below
Outputs:
- remapped: float32 [4, 128, 12, 128], P('level', 'dev')
- totals: float32 [12], replicated
Inputs may be any that keep to these rules, and one draw needn't show every extreme that they name: send_count[l, s, s] = 0; for every level some receiver device gets 2 live slots from every other device of the level. left_count[m, q, m] = 0; for every device index some receiver level gets 2 live slots from every other level. `own_weight`: nonnegative; entry [k, i] is zero where old cell k and new cell i differ by more than 3; each column sums to a positive intersect fraction of at most 1. `send_weight`: nonnegative; entry [k, i] is zero where old cell k and new cell i differ by more than 3; each column sums to a positive intersect fraction of at most 1. `left_weight`: nonnegative; entry [k, i] is zero where old cell k and new cell i differ by more than 3; each column sums to a positive intersect fraction of at most 1.
All inputs are finite; a program needn't handle non-finite values.
Results may differ from a plain program's by a relative error of at most 0.0045.
Values may be sent and summed in bfloat16 or wider, within the bound.
A program may use at most 64 MiB of HBM per device.

v0:
```python
import jax
import jax.numpy as jnp
from jax import lax
from jax.sharding import PartitionSpec as P


def pick_donors(rounded, block_index, count):
    donors = rounded[block_index]
    slots = block_index.shape[1]
    valid = lax.broadcasted_iota(jnp.int32, (1, slots), 1) < count[:, None]
    return jnp.where(valid[:, :, None, None], donors, jnp.zeros_like(donors))


def apply_weights(donors, weights):
    return jnp.einsum("pcmk,pcki->pcmi", donors, weights, preferred_element_type=jnp.float32)


def place_terms(contrib, target, blocks):
    comp = contrib.shape[2]
    cells = contrib.shape[3]
    flat_target = target.reshape(-1)
    onehot = (flat_target[:, None] == lax.broadcasted_iota(jnp.int32, (1, blocks), 1)).astype(
        jnp.float32
    )
    return jnp.einsum(
        "sb,smi->bmi", onehot, contrib.reshape(-1, comp, cells), precision=lax.Precision.HIGHEST
    )


def body(
    fields,
    own_src,
    own_weight,
    send_block,
    send_target,
    send_count,
    send_weight,
    left_block,
    left_target,
    left_count,
    left_weight,
):
    local = fields[0]
    blocks = local.shape[0]
    rounded = local.astype(jnp.bfloat16)
    own = jnp.einsum(
        "bmk,bki->bmi", rounded[own_src[0]], own_weight[0], preferred_element_type=jnp.float32
    )
    donors = pick_donors(rounded, send_block[0, 0], send_count[0, 0])
    strays = pick_donors(rounded, left_block[0, 0], left_count[0, 0])
    intra_terms, intra_target = (
        lax.all_to_all(
            apply_weights(donors, send_weight[0, 0]), "dev", split_axis=0, concat_axis=0, tiled=True
        ),
        lax.all_to_all(send_target[0, 0], "dev", split_axis=0, concat_axis=0, tiled=True),
    )
    left_terms, left_where = (
        lax.all_to_all(
            apply_weights(strays, left_weight[0, 0]),
            "level",
            split_axis=0,
            concat_axis=0,
            tiled=True,
        ),
        lax.all_to_all(left_target[0, 0], "level", split_axis=0, concat_axis=0, tiled=True),
    )
    remapped = (
        own
        + place_terms(intra_terms, intra_target, blocks)
        + place_terms(left_terms, left_where, blocks)
    )
    sums = lax.psum(jnp.sum(remapped, axis=(0, 2)), ("level", "dev"))
    totals = sums / (remapped.shape[2] * blocks)
    return (remapped[None], totals)


def solution(mesh):
    in_specs = (
        P("level", "dev", None, None),
        P("level", "dev"),
        P("level", "dev", None, None),
        P("level", "dev", None, None),
        P("level", "dev", None, None),
        P("level", "dev", None),
        P("level", "dev", None, None, None, None),
        P("level", "dev", None, None),
        P("level", "dev", None, None),
        P("level", "dev", None),
        P("level", "dev", None, None, None, None),
    )
    out_specs = (P("level", "dev", None, None), P())
    return jax.shard_map(body, mesh=mesh, in_specs=in_specs, out_specs=out_specs, check_vma=False)
```

profile of v0, /device:TPU:0, one launch (start us, length us, event | category | flops | bytes accessed | tf_op | source)
XLA Modules:
  0.0 84.1 jit_solution(18198775144529475194)
XLA Ops:
  0.6 0.0 copy-start
  0.6 0.0 copy-start.3
  0.7 0.0 copy-start.2
  0.7 0.0 copy-start.1
  0.7 0.7 copy-done.3
  1.4 0.6 copy.41
  2.0 6.3 %all-to-all-start.2 = ((s32[4,1,2]{2,1,0:T(1,128)}), s32[4,1,2]{2,1,0:T(1,128)S(1)}, u32[]{:S(2)}, u32[]{:S(2)}) async-start(s32[4,1,2]{2,1,0:T(1,128)} %copy.41), calls=%async_computation.2 | async-start | bytes 4096 | tf_op jit(solution)/shard_map/all_to_all | solution.py:65
  8.4 0.7 fusion.21
  9.0 0.7 iota_compare_fusion.3
  9.8 0.7 compare_select_fusion.1
  10.4 0.7 iota_compare_fusion.2
  11.2 0.7 compare_select_fusion
  11.9 0.1 copy.42
  11.9 0.1 reshape.173
  12.0 0.1 copy.37
  12.1 0.1 reshape.165
  12.2 1.3 %copy.36 = s32[8,1,2]{2,1,0:T(1,128)} copy(s32[8,1,2]{0,2,1:T(2,128)} %bitcast.53) | data formatting | bytes 128 | tf_op jit(solution)/shard_map/all_to_all | solution.py:55
  13.6 0.9 %copy.52 = bf16[1,16,12,128]{3,2,1,0:T(8,128)(2,1)S(1)} copy(f32[1,16,12,128]{3,1,2,0:T(8,128)} %param.11) | data formatting | bytes 147456 | tf_op args[0]
  14.5 0.6 gather_fusion.2
  15.1 0.6 gather_fusion.1
  15.6 0.0 copy-done.2
  15.6 0.2 fusion.4
  15.9 0.0 copy-done.1
  15.9 0.3 fusion.1
  16.2 0.0 all-to-all-done.2
  16.2 3.7 %all-to-all-start = ((s32[8,1,2]{2,1,0:T(1,128)}), s32[8,1,2]{2,1,0:T(1,128)S(1)}, u32[]{:S(2)}, u32[]{:S(2)}) async-start(s32[8,1,2]{2,1,0:T(1,128)} %copy.36), calls=%async_computation | async-start | bytes 8192 | tf_op jit(solution)/shard_map/all_to_all | solution.py:55
  19.9 0.6 copy.43
  20.6 4.0 %all-to-all-done = s32[8,1,2]{2,1,0:T(1,128)S(1)} async-done(((s32[8,1,2]{2,1,0:T(1,128)}), s32[8,1,2]{2,1,0:T(1,128)S(1)}, u32[]{:S(2)}, u32[]{:S(2)}) %all-to-all-start) | async-done | bytes 96 | tf_op jit(solution)/shard_map/all_to_all | solution.py:55
  24.5 5.1 %all-to-all-start.3 = ((f32[4,2,12,128]{3,1,2,0:T(2,128)}), f32[4,2,12,128]{3,1,2,0:T(2,128)S(1)}, u32[]{:S(2)}, u32[]{:S(2)}) async-start(f32[4,2,12,128]{3,1,2,0:T(2,128)} %copy.43), calls=%async_computation.3 | async-start | bytes 98304 | tf_op jit(solution)/shard_map/all_to_all | solution.py:58
  29.6 0.6 gather_fusion
  30.2 0.7 copy.38
  30.9 0.5 broadcast.122
  31.4 0.7 reduce.6
  32.1 0.1 eq.34
  32.2 0.7 reduce.7
  32.8 0.1 eq.30
  32.9 2.4 %all-to-all-done.3 = f32[4,2,12,128]{3,1,2,0:T(2,128)S(1)} async-done(((f32[4,2,12,128]{3,1,2,0:T(2,128)}), f32[4,2,12,128]{3,1,2,0:T(2,128)S(1)}, u32[]{:S(2)}, u32[]{:S(2)}) %all-to-all-start.3) | async-done | bytes 49184 | tf_op jit(solution)/shard_map/all_to_all | solution.py:58
  35.3 3.4 %all-to-all-start.1 = ((f32[8,2,12,128]{3,1,2,0:T(2,128)}), f32[8,2,12,128]{3,1,2,0:T(2,128)S(1)}, u32[]{:S(2)}, u32[]{:S(2)}) async-start(f32[8,2,12,128]{3,1,2,0:T(2,128)} %copy.38), calls=%async_computation.1 | async-start | bytes 196608 | tf_op jit(solution)/shard_map/all_to_all | solution.py:52
  38.7 0.3 fusion.18
  39.0 4.8 %all-to-all-done.1 = f32[8,2,12,128]{3,1,2,0:T(2,128)S(1)} async-done(((f32[8,2,12,128]{3,1,2,0:T(2,128)}), f32[8,2,12,128]{3,1,2,0:T(2,128)S(1)}, u32[]{:S(2)}, u32[]{:S(2)}) %all-to-all-start.1) | async-done | bytes 98336 | tf_op jit(solution)/shard_map/all_to_all | solution.py:52
  43.9 0.2 fusion.14
  44.1 0.0 copy-done
  44.1 0.4 fusion.24
  44.4 38.5 %psum.7 = f32[12]{0:T(128)S(1)} all-reduce(f32[12]{0:T(128)S(1)} %get-tuple-element.8), channel_id=1, replica_groups=mesh['level'=4,'dev'=8] {'level','dev'}, use_global_device_ids=true, to_apply=%region_1.2 | all-reduce | flops 12 | bytes 96 | tf_op jit(solution)/shard_map/psum | solution.py:72
  82.9 0.5 broadcast_multiply_fusion
  83.4 0.7 copy.46
  (5 shorter events, 0.1 us)
Async XLA Ops:
  0.6 43.4 %copy-start = (bf16[1,16,128,128]{3,2,1,0:T(8,128)(2,1)S(1)}, bf16[1,16,128,128]{3,2,1,0:T(8,128)(2,1)}, u32[]{:S(2)}) copy-start(bf16[1,16,128,128]{3,2,1,0:T(8,128)(2,1)} %param.13) | copy-start | bytes 1572868
  0.6 0.7 copy-start.3
  0.7 15.0 %copy-start.2 = (bf16[1,1,4,2,128,128]{5,4,3,2,1,0:T(8,128)(2,1)S(1)}, bf16[1,1,4,2,128,128]{5,4,3,2,1,0:T(8,128)(2,1)}, u32[]{:S(2)}) copy-start(bf16[1,1,4,2,128,128]{5,4,3,2,1,0:T(8,128)(2,1)} %param.21) | copy-start | bytes 786436
  0.7 15.2 %copy-start.1 = (bf16[1,1,8,2,128,128]{5,4,3,2,1,0:T(8,128)(2,1)S(1)}, bf16[1,1,8,2,128,128]{5,4,3,2,1,0:T(8,128)(2,1)}, u32[]{:S(2)}) copy-start(bf16[1,1,8,2,128,128]{5,4,3,2,1,0:T(8,128)(2,1)} %param.17) | copy-start | bytes 1572868
  2.0 14.2 %all-to-all-start.2 = ((s32[4,1,2]{2,1,0:T(1,128)}), s32[4,1,2]{2,1,0:T(1,128)S(1)}, u32[]{:S(2)}, u32[]{:S(2)}) async-start(s32[4,1,2]{2,1,0:T(1,128)} %copy.41), calls=%async_computation.2 | async-start | bytes 4096 | tf_op jit(solution)/shard_map/all_to_all | solution.py:65
  16.2 8.3 %all-to-all-start = ((s32[8,1,2]{2,1,0:T(1,128)}), s32[8,1,2]{2,1,0:T(1,128)S(1)}, u32[]{:S(2)}, u32[]{:S(2)}) async-start(s32[8,1,2]{2,1,0:T(1,128)} %copy.36), calls=%async_computation | async-start | bytes 8192 | tf_op jit(solution)/shard_map/all_to_all | solution.py:55
  24.5 10.8 %all-to-all-start.3 = ((f32[4,2,12,128]{3,1,2,0:T(2,128)}), f32[4,2,12,128]{3,1,2,0:T(2,128)S(1)}, u32[]{:S(2)}, u32[]{:S(2)}) async-start(f32[4,2,12,128]{3,1,2,0:T(2,128)} %copy.43), calls=%async_computation.3 | async-start | bytes 98304 | tf_op jit(solution)/shard_map/all_to_all | solution.py:58
  35.3 8.5 %all-to-all-start.1 = ((f32[8,2,12,128]{3,1,2,0:T(2,128)}), f32[8,2,12,128]{3,1,2,0:T(2,128)S(1)}, u32[]{:S(2)}, u32[]{:S(2)}) async-start(f32[8,2,12,128]{3,1,2,0:T(2,128)} %copy.38), calls=%async_computation.1 | async-start | bytes 196608 | tf_op jit(solution)/shard_map/all_to_all | solution.py:52
where the time goes:
time: 84.7 us; the launch traced here: 84.1 us
  blocking collectives  38.5 us (45%)
  starting transfers between devices  18.5 us (22%)
  waiting for transfers between devices  11.2 us (13%)
  local copies, waits for them, and re-layouts  8.43 us (10%)
  other arithmetic  5.33 us (6%)
  matrix products  1.38 us (2%)
    psum x1, blocking collectives, body(): sums = lax.psum(jnp.sum(remapped, axis=(0, 2)), ('level', 'dev'))  38.5 us
    all_to_all x1, starting transfers between devices, body(): lax.all_to_all(left_target[0, 0], 'level', split_axis=0, concat_axis=0, t...  6.35 us
    all_to_all x1, starting transfers between devices, body(): lax.all_to_all(apply_weights(strays, left_weight[0, 0]), 'level', split_a...  5.09 us
    all_to_all x1, waiting for transfers between devices, body(): lax.all_to_all(apply_weights(donors, send_weight[0, 0]), 'dev', split_axi...  4.79 us
    all_to_all x1, waiting for transfers between devices, body(): lax.all_to_all(send_target[0, 0], 'dev', split_axis=0, concat_axis=0, til...  3.97 us
    all_to_all x1, starting transfers between devices, body(): lax.all_to_all(send_target[0, 0], 'dev', split_axis=0, concat_axis=0, til...  3.74 us
    all_to_all x1, starting transfers between devices, body(): lax.all_to_all(apply_weights(donors, send_weight[0, 0]), 'dev', split_axi...  3.36 us
    all_to_all x1, waiting for transfers between devices, body(): lax.all_to_all(apply_weights(strays, left_weight[0, 0]), 'level', split_a...  2.42 us
  transfers between devices with their start and end apart: 4, of which 3 were waited for; matrix products, arithmetic and copies ran while one was open for 14% of the time, Pallas kernels for 0%

commit v1 on v0

--- a/solution.py
+++ b/solution.py
@@ -2,6 +2,29 @@
 import jax.numpy as jnp
 from jax import lax
 from jax.sharding import PartitionSpec as P
+
+
+def split_up(x, dim, size):
+    shape = x.shape
+    tiles = x.reshape(*shape[:dim], size, shape[dim] // size, *shape[dim + 1 :])
+    return jnp.moveaxis(tiles, dim, 0)
+
+
+def joined_along(parts, dim):
+    dims = list(parts.shape[1:])
+    dims[dim] *= parts.shape[0]
+    return jnp.moveaxis(parts, 0, dim).reshape(dims)
+
+
+def rotated_exchange(x, axis, split_dim, concat_dim):
+    size, here = (lax.axis_size(axis), lax.axis_index(axis))
+    tiles = split_up(x, split_dim, size)
+    finished = [tiles[here]]
+    for hop in range(1, size):
+        sent = tiles[(here + hop) % size]
+        finished.append(lax.ppermute(sent, axis, [(i, (i + hop) % size) for i in range(size)]))
+    tiles = jnp.stack(finished)[(here - jnp.arange(size)) % size]
+    return joined_along(tiles, concat_dim)
 
 
 def pick_donors(rounded, block_index, count):
@@ -55,13 +78,7 @@
         lax.all_to_all(send_target[0, 0], "dev", split_axis=0, concat_axis=0, tiled=True),
     )
     left_terms, left_where = (
-        lax.all_to_all(
-            apply_weights(strays, left_weight[0, 0]),
-            "level",
-            split_axis=0,
-            concat_axis=0,
-            tiled=True,
-        ),
+        rotated_exchange(apply_weights(strays, left_weight[0, 0]), "level", 0, 0),
         lax.all_to_all(left_target[0, 0], "level", split_axis=0, concat_axis=0, tiled=True),
     )
     remapped = (

time: 84.7 us -> 80.9 us (0.955)
  waiting for transfers between devices: 11.2 us -> 6.91 us
  blocking collectives: 38.5 us -> 40 us
  local copies, waits for them, and re-layouts: 8.43 us -> 7.48 us
    all_to_all x1 -> x0, starting transfers between devices: 5.09 us -> none  [body(): lax.all_to_all(apply_weights(strays, left_weight[0, 0]), 'level', split_a...]
    ppermute x0 -> x3, starting transfers between devices: none -> 5 us  [rotated_exchange(): lax.ppermute(sent, axis, [(i, (i + hop) % size) for i in range(size)])]
    all_to_all x1 -> x0, waiting for transfers between devices: 2.42 us -> none  [body(): lax.all_to_all(apply_weights(strays, left_weight[0, 0]), 'level', split_a...]
    psum x1, blocking collectives: 38.5 us -> 40 us  [body(): sums = lax.psum(jnp.sum(remapped, axis=(0, 2)), ('level', 'dev'))]
    all_to_all x1, waiting for transfers between devices: 4.79 us -> 3.47 us  [body(): lax.all_to_all(apply_weights(donors, send_weight[0, 0]), 'dev', split_axi...]
    unnamed x10 -> x14, local copies, waits for them, and re-layouts: 2.33 us -> 2.1 us
  transfers between devices with their start and end apart: 4 -> 6, of which waited for: 3 -> 2; matrix products, arithmetic and copies ran while one was open for 14% -> 13% of each run, Pallas kernels for 0% -> 0%
where the time goes in v1:
time: 80.9 us; the launch traced here: 80.4 us
  blocking collectives  40 us (49%)
  starting transfers between devices  18.4 us (23%)
  local copies, waits for them, and re-layouts  7.48 us (9%)
  waiting for transfers between devices  6.91 us (9%)
  other arithmetic  5.37 us (7%)
  matrix products  1.36 us (2%)
  between operations  0.82 us (1%)
    psum x1, blocking collectives, body(): sums = lax.psum(jnp.sum(remapped, axis=(0, 2)), ('level', 'dev'))  40 us
    all_to_all x1, starting transfers between devices, body(): lax.all_to_all(left_target[0, 0], 'level', split_axis=0, concat_axis=0, t...  6.35 us
    ppermute x3, starting transfers between devices, rotated_exchange(): lax.ppermute(sent, axis, [(i, (i + hop) % size) for i in range(size)])  5 us
    all_to_all x1, starting transfers between devices, body(): lax.all_to_all(send_target[0, 0], 'dev', split_axis=0, concat_axis=0, til...  3.72 us
    all_to_all x1, waiting for transfers between devices, body(): lax.all_to_all(apply_weights(donors, send_weight[0, 0]), 'dev', split_axi...  3.47 us
    all_to_all x1, waiting for transfers between devices, body(): lax.all_to_all(send_target[0, 0], 'dev', split_axis=0, concat_axis=0, til...  3.43 us
    all_to_all x1, starting transfers between devices, body(): lax.all_to_all(apply_weights(donors, send_weight[0, 0]), 'dev', split_axi...  3.36 us
    unnamed x14, local copies, waits for them, and re-layouts  2.1 us
  transfers between devices with their start and end apart: 6, of which 2 were waited for; matrix products, arithmetic and copies ran while one was open for 13% of the time, Pallas kernels for 0%

profile of v1, /device:TPU:0, one launch (start us, length us, event | category | flops | bytes accessed | tf_op | source)
XLA Modules:
  0.0 80.4 jit_solution(16269435124400279014)
XLA Ops:
  0.6 0.0 copy-start
  0.6 0.0 copy-start.4
  0.7 0.0 copy-start.3
  0.7 0.0 copy-start.2
  0.7 0.0 copy-start.1
  0.7 0.7 copy-done.4
  1.4 0.7 copy.41
  2.1 6.3 %all-to-all-start.2 = ((s32[4,1,2]{2,1,0:T(1,128)}), s32[4,1,2]{2,1,0:T(1,128)S(1)}, u32[]{:S(2)}, u32[]{:S(2)}) async-start(s32[4,1,2]{2,1,0:T(1,128)} %copy.41), calls=%async_computation.2 | async-start | bytes 4096 | tf_op jit(solution)/shard_map/all_to_all | solution.py:82
  8.4 0.7 iota_compare_fusion.3
  9.1 0.7 compare_select_fusion
  9.8 0.1 copy.42
  9.9 0.1 reshape.226
  10.0 0.0 copy-done.3
  10.1 0.6 gather_fusion.2
  10.6 0.0 copy-done.2
  10.6 0.2 fusion.4
  10.9 3.9 %collective-permute-start.2 = (f32[1,2,12,128]{3,2,1,0:T(8,128)S(1)}, f32[1,2,12,128]{3,2,1,0:T(8,128)S(1)}, u32[]{:S(2)}, u32[]{:S(2)}) collective-permute-start(f32[1,2,12,128]{3,2,1,0:T(8,128)S(1)} %get-tuple-element.9), channel_id=1, source_target_pairs={{0,24},{8,0},{16,8},{24,16},{1,25},{9,1},{17,9},{25,17},{2,26},{10... | collective-permute-start | bytes 36872 | tf_op jit(solution)/shard_map/ppermute | solution.py:25
  14.8 0.0 collective-permute-start.1
  14.8 1.1 %collective-permute-start = (f32[1,2,12,128]{3,2,1,0:T(8,128)S(1)}, f32[1,2,12,128]{3,2,1,0:T(8,128)S(1)}, u32[]{:S(2)}, u32[]{:S(2)}) collective-permute-start(f32[1,2,12,128]{3,2,1,0:T(8,128)S(1)} %get-tuple-element.11), channel_id=1, source_target_pairs={{0,8},{8,16},{16,24},{24,0},{1,9},{9,17},{17,25},{25,1},{2,10},{10... | collective-permute-start | bytes 36872 | tf_op jit(solution)/shard_map/ppermute | solution.py:25
  15.9 0.7 fusion.23
  16.6 0.7 compare_select_fusion.1
  17.3 0.7 iota_compare_fusion.2
  18.0 0.1 copy.37
  18.1 0.1 reshape.218
  18.2 0.6 gather_fusion.1
  18.7 0.0 copy-done.1
  18.7 0.3 fusion.1
  19.1 0.0 copy-start.5
  19.1 0.7 copy-done.5
  19.7 0.7 copy.36
  20.4 0.6 gather_fusion
  21.0 0.7 copy.38
  21.7 0.0 all-to-all-done.2
  21.7 3.7 %all-to-all-start = ((s32[8,1,2]{2,1,0:T(1,128)}), s32[8,1,2]{2,1,0:T(1,128)S(1)}, u32[]{:S(2)}, u32[]{:S(2)}) async-start(s32[8,1,2]{2,1,0:T(1,128)} %copy.36), calls=%async_computation | async-start | bytes 8192 | tf_op jit(solution)/shard_map/all_to_all | solution.py:78
  25.4 0.5 broadcast.194
  25.9 0.7 reduce.6
  26.6 0.1 eq.40
  26.7 3.4 %all-to-all-done = s32[8,1,2]{2,1,0:T(1,128)S(1)} async-done(((s32[8,1,2]{2,1,0:T(1,128)}), s32[8,1,2]{2,1,0:T(1,128)S(1)}, u32[]{:S(2)}, u32[]{:S(2)}) %all-to-all-start) | async-done | bytes 96 | tf_op jit(solution)/shard_map/all_to_all | solution.py:78
  30.1 3.4 %all-to-all-start.1 = ((f32[8,2,12,128]{3,1,2,0:T(2,128)}), f32[8,2,12,128]{3,1,2,0:T(2,128)S(1)}, u32[]{:S(2)}, u32[]{:S(2)}) async-start(f32[8,2,12,128]{3,1,2,0:T(2,128)} %copy.38), calls=%async_computation.1 | async-start | bytes 196608 | tf_op jit(solution)/shard_map/all_to_all | solution.py:75
  33.5 0.7 reduce.7
  34.1 0.1 eq.36
  34.2 0.0 collective-permute-done.2
  34.2 0.0 collective-permute-done.1
  34.2 0.0 collective-permute-done
  34.3 0.6 gather_fusion.3
  34.8 0.3 fusion.9
  35.1 3.5 %all-to-all-done.1 = f32[8,2,12,128]{3,1,2,0:T(2,128)S(1)} async-done(((f32[8,2,12,128]{3,1,2,0:T(2,128)}), f32[8,2,12,128]{3,1,2,0:T(2,128)S(1)}, u32[]{:S(2)}, u32[]{:S(2)}) %all-to-all-start.1) | async-done | bytes 98336 | tf_op jit(solution)/shard_map/all_to_all | solution.py:75
  38.6 0.2 fusion.16
  38.8 0.0 copy-done
  38.8 0.4 fusion.27
  39.2 40.0 %psum.7 = f32[12]{0:T(128)S(1)} all-reduce(f32[12]{0:T(128)S(1)} %get-tuple-element.12), channel_id=1, replica_groups=mesh['level'=4,'dev'=8] {'level','dev'}, use_global_device_ids=true, to_apply=%region_1.2 | all-reduce | flops 12 | bytes 96 | tf_op jit(solution)/shard_map/psum | solution.py:89
  79.2 0.5 broadcast_multiply_fusion
  79.8 0.7 copy.45
  (9 shorter events, 0.1 us)
Async XLA Ops:
  0.6 38.2 %copy-start = (bf16[1,16,128,128]{3,2,1,0:T(8,128)(2,1)S(1)}, bf16[1,16,128,128]{3,2,1,0:T(8,128)(2,1)}, u32[]{:S(2)}) copy-start(bf16[1,16,128,128]{3,2,1,0:T(8,128)(2,1)} %param.13) | copy-start | bytes 1572868
  0.6 0.7 copy-start.4
  0.7 9.4 %copy-start.3 = (f32[1,16,12,128]{3,1,2,0:T(8,128)S(1)}, f32[1,16,12,128]{3,1,2,0:T(8,128)}, u32[]{:S(2)}) copy-start(f32[1,16,12,128]{3,1,2,0:T(8,128)} %param.11) | copy-start | bytes 294916
  0.7 10.0 %copy-start.2 = (bf16[1,1,4,2,128,128]{5,4,3,2,1,0:T(8,128)(2,1)S(1)}, bf16[1,1,4,2,128,128]{5,4,3,2,1,0:T(8,128)(2,1)}, u32[]{:S(2)}) copy-start(bf16[1,1,4,2,128,128]{5,4,3,2,1,0:T(8,128)(2,1)} %param.21) | copy-start | bytes 786436
  0.7 18.1 %copy-start.1 = (bf16[1,1,8,2,128,128]{5,4,3,2,1,0:T(8,128)(2,1)S(1)}, bf16[1,1,8,2,128,128]{5,4,3,2,1,0:T(8,128)(2,1)}, u32[]{:S(2)}) copy-start(bf16[1,1,8,2,128,128]{5,4,3,2,1,0:T(8,128)(2,1)} %param.17) | copy-start | bytes 1572868
  2.1 19.6 %all-to-all-start.2 = ((s32[4,1,2]{2,1,0:T(1,128)}), s32[4,1,2]{2,1,0:T(1,128)S(1)}, u32[]{:S(2)}, u32[]{:S(2)}) async-start(s32[4,1,2]{2,1,0:T(1,128)} %copy.41), calls=%async_computation.2 | async-start | bytes 4096 | tf_op jit(solution)/shard_map/all_to_all | solution.py:82
  10.9 23.3 %collective-permute-start.2 = (f32[1,2,12,128]{3,2,1,0:T(8,128)S(1)}, f32[1,2,12,128]{3,2,1,0:T(8,128)S(1)}, u32[]{:S(2)}, u32[]{:S(2)}) collective-permute-start(f32[1,2,12,128]{3,2,1,0:T(8,128)S(1)} %get-tuple-element.9), channel_id=1, source_target_pairs={{0,24},{8,0},{16,8},{24,16},{1,25},{9,1},{17,9},{25,17},{2,26},{10... | collective-permute-start | bytes 36872 | tf_op jit(solution)/shard_map/ppermute | solution.py:25
  14.8 19.5 %collective-permute-start.1 = (f32[1,2,12,128]{3,2,1,0:T(8,128)S(1)}, f32[1,2,12,128]{3,2,1,0:T(8,128)S(1)}, u32[]{:S(2)}, u32[]{:S(2)}) collective-permute-start(f32[1,2,12,128]{3,2,1,0:T(8,128)S(1)} %get-tuple-element.10), channel_id=1, source_target_pairs={{0,16},{8,24},{16,0},{24,8},{1,17},{9,25},{17,1},{25,9},{2,18},{10... | collective-permute-start | bytes 36872 | tf_op jit(solution)/shard_map/ppermute | solution.py:25
  14.8 19.5 %collective-permute-start = (f32[1,2,12,128]{3,2,1,0:T(8,128)S(1)}, f32[1,2,12,128]{3,2,1,0:T(8,128)S(1)}, u32[]{:S(2)}, u32[]{:S(2)}) collective-permute-start(f32[1,2,12,128]{3,2,1,0:T(8,128)S(1)} %get-tuple-element.11), channel_id=1, source_target_pairs={{0,8},{8,16},{16,24},{24,0},{1,9},{9,17},{17,25},{25,1},{2,10},{10... | collective-permute-start | bytes 36872 | tf_op jit(solution)/shard_map/ppermute | solution.py:25
  19.1 0.7 copy-start.5
  21.7 8.4 %all-to-all-start = ((s32[8,1,2]{2,1,0:T(1,128)}), s32[8,1,2]{2,1,0:T(1,128)S(1)}, u32[]{:S(2)}, u32[]{:S(2)}) async-start(s32[8,1,2]{2,1,0:T(1,128)} %copy.36), calls=%async_computation | async-start | bytes 8192 | tf_op jit(solution)/shard_map/all_to_all | solution.py:78
  30.1 8.5 %all-to-all-start.1 = ((f32[8,2,12,128]{3,1,2,0:T(2,128)}), f32[8,2,12,128]{3,1,2,0:T(2,128)S(1)}, u32[]{:S(2)}, u32[]{:S(2)}) async-start(f32[8,2,12,128]{3,1,2,0:T(2,128)} %copy.38), calls=%async_computation.1 | async-start | bytes 196608 | tf_op jit(solution)/shard_map/all_to_all | solution.py:75
